TPU v7x, 32 devices: a whole 2x2x4 slice. The times are simulated.
32 devices in a mesh: narrow: 4 (over x, core), wide: 8 (over z, y).
Axes of the slice: x: 2, y: 2, z: 4, core: 2. Of those that a mesh axis runs over, the one named last changes fastest.
Arguments:
- block_ids: int32 [512, 4], P(('narrow', 'wide')), may hold values from 0 to 511, as said below
- incidence: int32 [512, 4, 128, 128], P(('narrow', 'wide')), may hold values from 0 to 1
- costs: int32 [512, 128], P(('narrow', 'wide')), may hold values from 16 to 80
- start_mult: float32 [512, 128], replicated, may hold values from 0.25 to 4
- upper: float32 [1], replicated, may hold values from 65536 to 131072
Outputs:
- multipliers: float32 [512, 128], replicated
- primal_mean: float32 [512, 128], P(('narrow', 'wide'))
Inputs may be any that keep to these rules, and one draw needn't show every extreme that they name: `block_ids`: the 4 row blocks listed for one tile are distinct.
All inputs are finite; a program needn't handle non-finite values.
Results may differ from a plain program's by a relative error of at most 0.0003.
Values sent between devices are 32-bit elements; how exact they have to be, the bound alone decides.
A program may use at most 64 MiB of HBM per device.

v0:
```python
import jax
import jax.numpy as jnp
from jax import lax
from jax.sharding import PartitionSpec as P

BLK = 128
K = 4
ITERS = 3


def local(block_ids, incidence, costs, start_mult, upper):
    hi = lax.Precision.HIGHEST
    tiles_here = block_ids.shape[0]
    blocks = start_mult.shape[0]
    incf = incidence.astype(jnp.float32)
    costf = costs.astype(jnp.float32)
    onehot = (
        block_ids.reshape(tiles_here * K, 1) == jnp.arange(blocks, dtype=jnp.int32)[None, :]
    ).astype(jnp.float32)
    count_narrow = lax.axis_size("narrow")
    count_wide = lax.axis_size("wide")
    share_rows = blocks // lax.axis_size(("narrow", "wide"))
    share_start = lax.axis_index(("narrow", "wide")) * share_rows
    mult = start_mult
    primal_mean = jnp.zeros(costs.shape, jnp.float32)
    for step in range(ITERS):
        u_tile = jnp.take(mult, block_ids, axis=0)
        reduced = costf - jnp.einsum("tkrc,tkr->tc", incf, u_tile, precision=hi)
        primal = 1.0 / (1.0 + jnp.exp(reduced / 8.0))
        local_soft = jnp.sum(-8.0 * jax.nn.softplus(-reduced / 8.0))
        if step == 0:
            primal_mean = primal
        else:
            primal_mean = 0.3 * primal + 0.7 * primal_mean
        part = jnp.einsum("tkrc,tc->tkr", incf, primal_mean, precision=hi).reshape(
            tiles_here * K, BLK
        )
        row_part = jnp.dot(onehot.T, part, precision=hi, preferred_element_type=jnp.float32)
        outgoing = row_part.reshape(count_narrow, count_wide, share_rows, BLK)
        incoming = lax.all_to_all(
            lax.all_to_all(outgoing, "narrow", split_axis=0, concat_axis=0, tiled=True),
            "wide",
            split_axis=1,
            concat_axis=1,
            tiled=True,
        )
        cover_share = jnp.sum(jnp.sum(incoming, axis=0), axis=0)
        mult_share = lax.dynamic_slice_in_dim(mult, share_start, share_rows, 0)
        slope = 1.0 - cover_share
        norm, mult_total, late_sum = lax.psum(
            (jnp.sum(slope * slope), jnp.sum(mult_share), local_soft), ("narrow", "wide")
        )
        value = mult_total + late_sum
        size = (upper[0] - value) / (norm + 1e-06)
        new_share = jnp.maximum(0.0, mult_share + size * slope)
        mult = lax.all_gather(new_share, ("narrow", "wide"), axis=0, tiled=True)
    return (mult, primal_mean)


def solution(mesh):
    in_specs = (
        P(("narrow", "wide"), None),
        P(("narrow", "wide"), None, None, None),
        P(("narrow", "wide"), None),
        P(),
        P(),
    )
    out_specs = (P(), P(("narrow", "wide"), None))
    return jax.shard_map(local, mesh=mesh, in_specs=in_specs, out_specs=out_specs, check_vma=False)
```

profile of v0, /device:TPU:0, one launch (start us, length us, event | category | flops | bytes accessed | tf_op | source)
XLA Modules:
  0.0 426.2 jit_solution(1178383881923371404)
XLA Ops:
  2.0 0.8 copy.23
  3.2 1.6 gather_fusion
  4.8 4.1 fusion.10
  9.6 3.4 fusion.8
  13.3 10.0 %all_to_all.30 = f32[4,8,16,128]{3,2,1,0:T(8,128)S(1)} all-to-all(f32[4,8,16,128]{3,2,1,0:T(8,128)S(1)} %fusion.16), channel_id=1, replica_groups=mesh['narrow'=4,'wide'=8] {'narrow'}, dimensions={0} | all-to-all | bytes 524288 | tf_op jit(solution)/shard_map/all_to_all | solution.py:41
  24.1 5.8 %all-to-all-start.1 = ((f32[4,8,16,128]{3,2,0,1:T(8,128)}), f32[4,8,16,128]{3,2,0,1:T(8,128)S(1)}, u32[]{:S(2)}, u32[]{:S(2)}) async-start(f32[4,8,16,128]{3,2,0,1:T(8,128)} %copy.24), calls=%async_computation.1 | async-start | bytes 524288 | tf_op jit(solution)/shard_map/all_to_all | solution.py:40
  29.9 1.4 dynamic-slice_reduce_fusion.2
  32.6 5.8 %all-to-all-done.1 = f32[4,8,16,128]{3,2,0,1:T(8,128)S(1)} async-done(((f32[4,8,16,128]{3,2,0,1:T(8,128)}), f32[4,8,16,128]{3,2,0,1:T(8,128)S(1)}, u32[]{:S(2)}, u32[]{:S(2)}) %all-to-all-start.1) | async-done | bytes 262176 | tf_op jit(solution)/shard_map/all_to_all | solution.py:40
  39.7 39.0 %all-reduce.2 = (f32[]{:T(128)}, f32[]{:T(128)}) all-reduce(f32[]{:T(128)S(6)} %add.95, f32[]{:T(128)} %multiply_reduce_fusion.2), channel_id=1, replica_groups=mesh['narrow'=4,'wide'=8] {'narrow','wide'}, use_global_device_ids=true, to_apply=%region_1.2 | all-reduce | flops 2 | bytes 16 | tf_op jit(solution)/shard_map/psum | solution.py:50
  80.8 67.3 %all_gather.9 = f32[512,128]{1,0:T(8,128)S(1)} all-gather(f32[16,128]{1,0:T(8,128)S(1)} %add_maximum_fusion.2), channel_id=1, replica_groups=mesh['narrow'=4,'wide'=8] {'narrow','wide'}, dimensions={0}, use_global_device_ids=true | all-gather | bytes 270336 | tf_op jit(solution)/shard_map/all_gather | solution.py:56
  148.8 4.1 fusion.6
  153.5 3.4 fusion.4
  157.3 8.4 %all_to_all.31 = f32[4,8,16,128]{3,2,1,0:T(8,128)S(1)} all-to-all(f32[4,8,16,128]{3,2,1,0:T(8,128)S(1)} %fusion.14), channel_id=1, replica_groups=mesh['narrow'=4,'wide'=8] {'narrow'}, dimensions={0} | all-to-all | bytes 524288 | tf_op jit(solution)/shard_map/all_to_all | solution.py:41
  166.4 3.4 all-to-all-start.3
  171.6 7.0 %all-to-all-done.3 = f32[4,8,16,128]{3,2,0,1:T(8,128)S(1)} async-done(((f32[4,8,16,128]{3,2,0,1:T(8,128)}), f32[4,8,16,128]{3,2,0,1:T(8,128)S(1)}, u32[]{:S(2)}, u32[]{:S(2)}) %all-to-all-start.3) | async-done | bytes 262176 | tf_op jit(solution)/shard_map/all_to_all | solution.py:40
  179.2 38.9 %all-reduce.1 = (f32[]{:T(128)}, f32[]{:T(128)}) all-reduce(f32[]{:T(128)S(6)} %add.100, f32[]{:T(128)} %multiply_reduce_fusion.1), channel_id=1, replica_groups=mesh['narrow'=4,'wide'=8] {'narrow','wide'}, use_global_device_ids=true, to_apply=%region_8.10 | all-reduce | flops 2 | bytes 16 | tf_op jit(solution)/shard_map/psum | solution.py:50
  219.5 67.5 %all_gather.10 = f32[512,128]{1,0:T(8,128)S(1)} all-gather(f32[16,128]{1,0:T(8,128)S(1)} %add_maximum_fusion.1), channel_id=1, replica_groups=mesh['narrow'=4,'wide'=8] {'narrow','wide'}, dimensions={0}, use_global_device_ids=true | all-gather | bytes 270336 | tf_op jit(solution)/shard_map/all_gather | solution.py:56
  287.6 4.1 fusion.2
  292.4 3.4 fusion
  296.1 8.4 %all_to_all.32 = f32[4,8,16,128]{3,2,1,0:T(8,128)S(1)} all-to-all(f32[4,8,16,128]{3,2,1,0:T(8,128)S(1)} %fusion.12), channel_id=1, replica_groups=mesh['narrow'=4,'wide'=8] {'narrow'}, dimensions={0} | all-to-all | bytes 524288 | tf_op jit(solution)/shard_map/all_to_all | solution.py:41
  305.2 3.4 all-to-all-start.5
  310.5 6.9 %all-to-all-done.5 = f32[4,8,16,128]{3,2,0,1:T(8,128)S(1)} async-done(((f32[4,8,16,128]{3,2,0,1:T(8,128)}), f32[4,8,16,128]{3,2,0,1:T(8,128)S(1)}, u32[]{:S(2)}, u32[]{:S(2)}) %all-to-all-start.5) | async-done | bytes 262176 | tf_op jit(solution)/shard_map/all_to_all | solution.py:40
  318.1 38.9 %all-reduce = (f32[]{:T(128)}, f32[]{:T(128)}) all-reduce(f32[]{:T(128)S(6)} %add.106, f32[]{:T(128)} %multiply_reduce_fusion), channel_id=1, replica_groups=mesh['narrow'=4,'wide'=8] {'narrow','wide'}, use_global_device_ids=true, to_apply=%region_15.17 | all-reduce | flops 2 | bytes 16 | tf_op jit(solution)/shard_map/psum | solution.py:50
  358.3 67.3 %all_gather.11 = f32[512,128]{1,0:T(8,128)S(1)} all-gather(f32[16,128]{1,0:T(8,128)S(1)} %add_maximum_fusion), channel_id=1, replica_groups=mesh['narrow'=4,'wide'=8] {'narrow','wide'}, dimensions={0}, use_global_device_ids=true | all-gather | bytes 270336 | tf_op jit(solution)/shard_map/all_gather | solution.py:56
  (44 shorter events, 12.9 us)
Async XLA Ops:
  0.6 8.3 %copy-start.3 = (s32[16,128]{1,0:T(8,128)S(1)}, s32[16,128]{1,0:T(8,128)}, u32[]{:S(2)}) copy-start(s32[16,128]{1,0:T(8,128)} %param.9) | copy-start | bytes 24580
  4.7 4.9 %copy-start = (s32[16,4,128,128]{3,2,1,0:T(8,128)S(1)}, s32[16,4,128,128]{3,2,1,0:T(8,128)}, u32[]{:S(2)}) copy-start(s32[16,4,128,128]{3,2,1,0:T(8,128)} %param.8) | copy-start | bytes 12582916
  24.1 14.4 %all-to-all-start.1 = ((f32[4,8,16,128]{3,2,0,1:T(8,128)}), f32[4,8,16,128]{3,2,0,1:T(8,128)S(1)}, u32[]{:S(2)}, u32[]{:S(2)}) async-start(f32[4,8,16,128]{3,2,0,1:T(8,128)} %copy.24), calls=%async_computation.1 | async-start | bytes 524288 | tf_op jit(solution)/shard_map/all_to_all | solution.py:40
  148.7 4.8 %copy-start.1 = (s32[16,4,128,128]{3,2,1,0:T(8,128)S(1)}, s32[16,4,128,128]{3,2,1,0:T(8,128)}, u32[]{:S(2)}) copy-start(s32[16,4,128,128]{3,2,1,0:T(8,128)} %param.8) | copy-start | bytes 12582916
  166.4 12.2 %all-to-all-start.3 = ((f32[4,8,16,128]{3,2,0,1:T(8,128)}), f32[4,8,16,128]{3,2,0,1:T(8,128)S(1)}, u32[]{:S(2)}, u32[]{:S(2)}) async-start(f32[4,8,16,128]{3,2,0,1:T(8,128)} %copy.27), calls=%async_computation.3 | async-start | bytes 524288 | tf_op jit(solution)/shard_map/all_to_all | solution.py:40
  287.5 4.8 %copy-start.2 = (s32[16,4,128,128]{3,2,1,0:T(8,128)S(1)}, s32[16,4,128,128]{3,2,1,0:T(8,128)}, u32[]{:S(2)}) copy-start(s32[16,4,128,128]{3,2,1,0:T(8,128)} %param.8) | copy-start | bytes 12582916
  292.4 133.9 %copy-start.4 = (f32[16,128]{1,0:T(8,128)}, f32[16,128]{1,0:T(8,128)S(1)}, u32[]{:S(2)}) copy-start(f32[16,128]{1,0:T(8,128)S(1)} %get-tuple-element.18) | copy-start | bytes 24580
  305.2 12.2 %all-to-all-start.5 = ((f32[4,8,16,128]{3,2,0,1:T(8,128)}), f32[4,8,16,128]{3,2,0,1:T(8,128)S(1)}, u32[]{:S(2)}, u32[]{:S(2)}) async-start(f32[4,8,16,128]{3,2,0,1:T(8,128)} %copy.30), calls=%async_computation.5 | async-start | bytes 524288 | tf_op jit(solution)/shard_map/all_to_all | solution.py:40
where the time goes:
time: 427 us; the launch traced here: 426 us
  blocking collectives  346 us (81%)
  matrix products  23.5 us (6%)
  waiting for transfers between devices  19.7 us (5%)
  starting transfers between devices  12.7 us (3%)
  between operations  9.14 us (2%)
  other arithmetic  8.77 us (2%)
  local copies, waits for them, and re-layouts  6.75 us (2%)
    all_gather x3, blocking collectives, local(): mult = lax.all_gather(new_share, ('narrow', 'wide'), axis=0, tiled=True)  202 us
    psum x3, blocking collectives, local(): lax.psum((jnp.sum(slope * slope), jnp.sum(mult_share), local_soft), ('nar...  117 us
    all_to_all x3, blocking collectives, local(): lax.all_to_all(outgoing, 'narrow', split_axis=0, concat_axis=0, tiled=True)  26.8 us
    all_to_all x3, waiting for transfers between devices, local(): lax.all_to_all(lax.all_to_all(outgoing, 'narrow', split_axis=0, concat_ax...  19.7 us
    all_to_all x3, starting transfers between devices, local(): lax.all_to_all(lax.all_to_all(outgoing, 'narrow', split_axis=0, concat_ax...  12.7 us
    dot_general x3, matrix products, local(): reduced = costf - jnp.einsum('tkrc,tkr->tc', incf, u_tile, precision=hi)  12.3 us
    dot_general x3, matrix products, local(): jnp.einsum('tkrc,tc->tkr', incf, primal_mean, precision=hi)  10.2 us
  transfers between devices with their start and end apart: 3, of which 3 were waited for; matrix products, arithmetic and copies ran while one was open for 1% of the time, Pallas kernels for 0%

commit v1 on v0

v1 whole, which is shorter than its diff:
```python
import functools

import jax
import jax.numpy as jnp
from jax import lax
from jax.experimental import pallas as pl
from jax.experimental.pallas import tpu as pltpu
from jax.sharding import PartitionSpec as P

ITERS = 3
MESH = pl.DeviceIdType.MESH


def pieces(x):
    hi = x.astype(jnp.bfloat16)
    rest = x - hi.astype(jnp.float32)
    mid = rest.astype(jnp.bfloat16)
    lo = (rest - mid.astype(jnp.float32)).astype(jnp.bfloat16)
    return jnp.concatenate([hi, mid, lo], axis=0)


def fold(x):
    rows = x.shape[0] // 3
    return x[:rows] + x[rows : 2 * rows] + x[2 * rows :]


def kernel(
    narrow, wide, ids, inc, costs, start, upper,
    mult_out, mean_out,
    inc_buf, w, u, onehot, outgoing, incoming, share_src, cover, soft_src, soft_buf,
    load_sem, rs_send, rs_recv, ag_send, ag_recv, soft_send, soft_recv,
):
    n = narrow * wide
    tiles, k_count, blk, cols = inc.shape
    share = cover.shape[1]
    blocks = n * share
    pairs = tiles // 2
    depth = k_count * blk
    me = lax.axis_index("narrow") * wide + lax.axis_index("wide")
    unroll = n <= 32

    def device(d):
        return (d // wide, d % wide)

    def to_others(act):
        def one(i, carry):
            act((me + i) % n)
            return carry

        if unroll:
            for i in range(1, n):
                one(i, 0)
        else:
            lax.fori_loop(1, n, one, 0)

    def wait_all(ref, sem):
        part = ref.at[pl.ds(0, n - 1)]
        pltpu.make_async_copy(part, part, sem).wait()

    loads = []
    for p in range(pairs):
        copy = pltpu.make_async_copy(
            inc.at[pl.ds(2 * p, 2)], inc_buf.at[pl.ds(2 * p, 2)], load_sem.at[p]
        )
        copy.start()
        loads.append(copy)

    barrier = pltpu.get_barrier_semaphore()
    to_others(lambda d: pl.semaphore_signal(barrier, inc=1, device_id=device(d), device_id_type=MESH))

    u[...] = start[...]
    count = tiles * k_count
    lane = lax.broadcasted_iota(jnp.int32, (1, 3 * count), 1) % count
    listed = jnp.zeros((1, 3 * count), jnp.int32)
    for t in range(tiles):
        for k in range(k_count):
            listed = jnp.where(lane == k * tiles + t, ids[t, k], listed)
    row = lax.broadcasted_iota(jnp.int32, (blocks, 3 * count), 0)
    onehot[...] = (row == listed).astype(jnp.float32).astype(jnp.bfloat16)

    costf = costs[...].astype(jnp.float32)
    tile_row = lax.broadcasted_iota(jnp.int32, (tiles, cols), 0)
    tile_row_wide = lax.broadcasted_iota(jnp.int32, (tiles, depth), 0)
    mean = None
    for step in range(ITERS):
        rows = []
        for t in range(tiles):
            cells = []
            for k in range(k_count):
                b = ids[t, k]
                cells.append(u[b // share, pl.ds(b % share, 1), :])
            rows.append(jnp.concatenate(cells, axis=1))
        lhs = pieces(jnp.concatenate(rows, axis=0))
        total = jnp.zeros((tiles, cols), jnp.float32)
        for p in range(pairs):
            if step == 0:
                loads[p].wait()
                for half in range(2):
                    w[p, :, half * cols : (half + 1) * cols] = (
                        inc_buf[2 * p + half].reshape(depth, cols).astype(jnp.float32).astype(jnp.bfloat16)
                    )
            got = fold(jnp.dot(lhs, w[p], preferred_element_type=jnp.float32))
            total = jnp.where(tile_row == 2 * p, got[:, :cols], total)
            total = jnp.where(tile_row == 2 * p + 1, got[:, cols:], total)
        reduced = costf - total
        scaled = reduced * 0.125
        primal = 1.0 / (1.0 + jnp.exp(scaled))
        soft = -8.0 * (jnp.maximum(-scaled, 0.0) + jnp.log1p(jnp.exp(-jnp.abs(scaled))))
        soft_row = jnp.sum(soft, axis=0, keepdims=True)
        soft_src[step] = soft_row
        soft_buf[step, me] = soft_row
        if step == 0:
            pl.semaphore_wait(barrier, n - 1)
        to_others(
            lambda d: pltpu.make_async_remote_copy(
                src_ref=soft_src.at[step], dst_ref=soft_buf.at[step, me],
                send_sem=soft_send.at[step], recv_sem=soft_recv.at[step],
                device_id=device(d), device_id_type=MESH,
            ).start()
        )
        mean = primal if step == 0 else 0.3 * primal + 0.7 * mean
        even = tile_row % 2 == 0
        lhs = pieces(
            jnp.concatenate([jnp.where(even, mean, 0.0), jnp.where(even, 0.0, mean)], axis=1)
        )
        part = jnp.zeros((tiles, depth), jnp.float32)
        for p in range(pairs):
            got = fold(
                lax.dot_general(
                    lhs, w[p], (((1,), (1,)), ((), ())), preferred_element_type=jnp.float32
                )
            )
            part = jnp.where(tile_row_wide // 2 == p, got, part)
        part = jnp.concatenate([part[:, k * blk : (k + 1) * blk] for k in range(k_count)], axis=0)
        mine = jnp.dot(onehot[...], pieces(part), preferred_element_type=jnp.float32)
        if step > 0:
            wait_all(outgoing, rs_send)
        outgoing[...] = mine.reshape(n, share, blk)
        to_others(
            lambda d: pltpu.make_async_remote_copy(
                src_ref=outgoing.at[d], dst_ref=incoming.at[me],
                send_sem=rs_send, recv_sem=rs_recv,
                device_id=device(d), device_id_type=MESH,
            ).start()
        )
        if step > 0:
            wait_all(cover, ag_send)
        incoming[me] = outgoing[me]
        wait_all(incoming, rs_recv)
        owned = jnp.sum(incoming[...], axis=0)
        share_src[...] = owned
        cover[me] = owned
        to_others(
            lambda d: pltpu.make_async_remote_copy(
                src_ref=share_src, dst_ref=cover.at[me],
                send_sem=ag_send, recv_sem=ag_recv,
                device_id=device(d), device_id_type=MESH,
            ).start()
        )
        wait_all(soft_buf.at[step], soft_recv.at[step])
        value = jnp.sum(u[...]) + jnp.sum(soft_buf[step])
        wait_all(cover, ag_recv)
        slope = 1.0 - cover[...]
        norm = jnp.sum(slope * slope)
        size = (jnp.full((1, 1, blk), upper[0] - value)) / (norm + 1e-06)
        new = jnp.maximum(0.0, u[...] + size * slope)
        if step < ITERS - 1:
            u[...] = new
        else:
            mult_out[...] = new
            mean_out[...] = mean
    wait_all(outgoing, rs_send)
    wait_all(cover, ag_send)
    for step in range(ITERS):
        wait_all(soft_buf.at[step], soft_send.at[step])


def local(narrow, wide, block_ids, incidence, costs, start_mult, upper):
    n = narrow * wide
    tiles, k_count, blk, cols = incidence.shape
    blocks = start_mult.shape[0]
    share = blocks // n
    vmem = pl.BlockSpec(memory_space=pltpu.VMEM)
    smem = pl.BlockSpec(memory_space=pltpu.SMEM)
    rows = (n, share, blk)
    mult, mean = pl.pallas_call(
        functools.partial(kernel, narrow, wide),
        name="volume",
        out_shape=(
            jax.ShapeDtypeStruct(rows, jnp.float32),
            jax.ShapeDtypeStruct(costs.shape, jnp.float32),
        ),
        in_specs=[smem, pl.BlockSpec(memory_space=pl.ANY), vmem, vmem, smem],
        out_specs=(vmem, vmem),
        scratch_shapes=[
            pltpu.VMEM(incidence.shape, jnp.int32),
            pltpu.VMEM((tiles // 2, k_count * blk, 2 * cols), jnp.bfloat16),
            pltpu.VMEM(rows, jnp.float32),
            pltpu.VMEM((blocks, 3 * tiles * k_count), jnp.bfloat16),
            pltpu.VMEM(rows, jnp.float32),
            pltpu.VMEM(rows, jnp.float32),
            pltpu.VMEM(rows[1:], jnp.float32),
            pltpu.VMEM(rows, jnp.float32),
            pltpu.VMEM((ITERS, 1, cols), jnp.float32),
            pltpu.VMEM((ITERS, n, 1, cols), jnp.float32),
            pltpu.SemaphoreType.DMA((tiles // 2,)),
            pltpu.SemaphoreType.DMA,
            pltpu.SemaphoreType.DMA,
            pltpu.SemaphoreType.DMA,
            pltpu.SemaphoreType.DMA,
            pltpu.SemaphoreType.DMA((ITERS,)),
            pltpu.SemaphoreType.DMA((ITERS,)),
        ],
        compiler_params=pltpu.CompilerParams(collective_id=0, has_side_effects=True),
    )(block_ids, incidence, costs, start_mult.reshape(rows), upper)
    return mult.reshape(blocks, blk), mean


def solution(mesh):
    in_specs = (
        P(("narrow", "wide"), None),
        P(("narrow", "wide"), None, None, None),
        P(("narrow", "wide"), None),
        P(),
        P(),
    )
    out_specs = (P(), P(("narrow", "wide"), None))
    body = functools.partial(local, mesh.shape["narrow"], mesh.shape["wide"])
    return jax.shard_map(body, mesh=mesh, in_specs=in_specs, out_specs=out_specs, check_vma=False)
```

time: 427 us -> 68.2 us (0.16)
  blocking collectives: 346 us -> 0 us
  Pallas kernels: 0 us -> 62.3 us
  matrix products: 23.5 us -> 0 us
  waiting for transfers between devices: 19.7 us -> 0 us
  starting transfers between devices: 12.7 us -> 0 us
  other arithmetic: 8.77 us -> 0 us
  between operations: 9.14 us -> 1.29 us
    all_gather x3 -> x0, blocking collectives: 202 us -> none  [local(): mult = lax.all_gather(new_share, ('narrow', 'wide'), axis=0, tiled=True)]
    psum x3 -> x0, blocking collectives: 117 us -> none  [local(): lax.psum((jnp.sum(slope * slope), jnp.sum(mult_share), local_soft), ('nar...]
    pallas_call x0 -> x1, Pallas kernels: none -> 62.3 us  [local(): pl.pallas_call(functools.partial(kernel, narrow, wide), name='volume', ou...]
    all_to_all x3 -> x0, blocking collectives: 26.8 us -> none  [local(): lax.all_to_all(outgoing, 'narrow', split_axis=0, concat_axis=0, tiled=True)]
    dot_general x9 -> x0, matrix products: 23.5 us -> none  [the longest x3 12.3 us: local(): reduced = costf - jnp.einsum('tkrc,tkr->tc', incf, u_tile, precision=hi)]
    all_to_all x3 -> x0, waiting for transfers between devices: 19.7 us -> none  [local(): lax.all_to_all(lax.all_to_all(outgoing, 'narrow', split_axis=0, concat_ax...]
    all_to_all x3 -> x0, starting transfers between devices: 12.7 us -> none  [local(): lax.all_to_all(lax.all_to_all(outgoing, 'narrow', split_axis=0, concat_ax...]
    reduce_sum x12 -> x0, other arithmetic: 6.4 us -> none  [the longest x3 2.62 us: local(): jnp.sum(mult_share)]
  transfers between devices with their start and end apart: 3 -> 0, of which waited for: 3 -> 0; matrix products, arithmetic and copies ran while one was open for 1% -> 0% of each run, Pallas kernels for 0% -> 0%
where the time goes in v1:
time: 68.2 us; the launch traced here: 67.9 us
  Pallas kernels  62.3 us (91%)
  local copies, waits for them, and re-layouts  4.32 us (6%)
  between operations  1.29 us (2%)
    pallas_call x1, Pallas kernels, local(): pl.pallas_call(functools.partial(kernel, narrow, wide), name='volume', ou...  62.3 us
    unnamed x3, local copies, waits for them, and re-layouts  4.32 us

profile of v1, /device:TPU:0, one launch (start us, length us, event | category | flops | bytes accessed | tf_op | source)
XLA Modules:
  0.0 67.9 jit_solution(3001640235669164207)
XLA Ops:
  1.3 1.4 %copy.7.ids = s32[16,4]{1,0:T(8,128)} copy(s32[16,4]{0,1:T(4,128)} %param.5) | data formatting | bytes 512 | tf_op args[0]
  2.6 62.3 %volume.1 = (f32[32,16,128]{2,1,0:T(8,128)}, f32[16,128]{1,0:T(8,128)}) custom-call(s32[16,4]{1,0:T(8,128)} %copy.7.ids, s32[16,4,128,128]{3,2,1,0:T(8,128)} %inc.1, s32[16,128]{1,0:T(8,128)} %costs.1, f32[32,16,128]{2,1,0:T(8,128)} %bitcast.2, f32[1]{0:T(128)S(6)} %copy.10.upper), custom_call_target="tpu_custom_call" | custom-call | tf_op jit(solution)/shard_map/volume/pallas_call | solution.py:186
  64.9 1.7 %copy.11 = f32[512,128]{1,0:T(8,128)} copy(f32[512,128]{1,0:T(8,128)} %bitcast.3) | data formatting | bytes 524288
  66.6 1.3 %copy.12 = f32[16,128]{1,0:T(8,128)} copy(f32[16,128]{1,0:T(8,128)} %get-tuple-element.9) | data formatting | bytes 16384

commit v2 on v1

v2 whole, which is shorter than its diff:
```python
import functools

import jax
import jax.numpy as jnp
from jax import lax
from jax.experimental import pallas as pl
from jax.experimental.pallas import tpu as pltpu
from jax.sharding import PartitionSpec as P

ITERS = 3
MESH = pl.DeviceIdType.MESH


def pieces(x):
    hi = x.astype(jnp.bfloat16)
    rest = x - hi.astype(jnp.float32)
    mid = rest.astype(jnp.bfloat16)
    lo = (rest - mid.astype(jnp.float32)).astype(jnp.bfloat16)
    return jnp.concatenate([hi, mid, lo], axis=0)


def fold(x):
    rows = x.shape[0] // 3
    return x[:rows] + x[rows : 2 * rows] + x[2 * rows :]


def kernel(
    narrow, wide, ids, inc, costs, start, upper,
    mult_out, mean_out,
    inc_buf, w, u, onehot, other_onehot, outgoing, incoming, cover,
    part_src, part_other, list_src, list_other, soft_src, soft_buf,
    load_sem, rs_send, rs_recv, ag_send, ag_recv, soft_send, soft_recv, pair_send, pair_recv,
):
    tiles, k_count, blk, cols = inc.shape
    share = cover.shape[1]
    chips = narrow * wide // 2
    half = chips * share
    pairs = tiles // 2
    depth = k_count * blk
    count = tiles * k_count
    across, along = lax.axis_index("narrow"), lax.axis_index("wide")
    core = across % 2
    me = (across // 2) * wide + along
    partner = (across + 1 - 2 * core, along)
    base = core * chips
    other_base = chips - base

    def to_others(act):
        def one(i, carry):
            d = (me + i) % chips
            act(d, ((d // wide) * 2 + core, d % wide))
            return carry

        if chips <= 16:
            for i in range(1, chips):
                one(i, 0)
        else:
            lax.fori_loop(1, chips, one, 0)

    def wait_all(ref, sem):
        part = ref.at[pl.ds(0, chips - 1)]
        pltpu.make_async_copy(part, part, sem).wait()

    def to_partner(src, dst, i):
        return pltpu.make_async_remote_copy(
            src_ref=src, dst_ref=dst, send_sem=pair_send.at[i], recv_sem=pair_recv.at[i],
            device_id=partner, device_id_type=MESH,
        )

    loads = []
    for p in range(pairs):
        copy = pltpu.make_async_copy(
            inc.at[pl.ds(2 * p, 2)], inc_buf.at[pl.ds(2 * p, 2)], load_sem.at[p]
        )
        copy.start()
        loads.append(copy)

    barrier = pltpu.get_barrier_semaphore()
    pl.semaphore_signal(barrier, inc=1, device_id=partner, device_id_type=MESH)
    to_others(
        lambda d, where: pl.semaphore_signal(barrier, inc=1, device_id=where, device_id_type=MESH)
    )

    u[...] = start[...]
    lane = lax.broadcasted_iota(jnp.int32, list_src.shape, 1) % count
    listed = jnp.zeros(list_src.shape, jnp.int32)
    for t in range(tiles):
        for k in range(k_count):
            listed = jnp.where(lane == k * tiles + t, ids[k, t], listed)
    listed = listed.astype(jnp.float32)
    list_src[...] = listed
    row = (lax.broadcasted_iota(jnp.int32, onehot.shape, 0) + core * half).astype(jnp.float32)

    def mark(names):
        return (row == names[:, : 3 * count]).astype(jnp.float32).astype(jnp.bfloat16)

    onehot[...] = mark(listed)

    costf = costs[...].astype(jnp.float32)
    tile_row = lax.broadcasted_iota(jnp.int32, (tiles, cols), 0)
    tile_row_wide = lax.broadcasted_iota(jnp.int32, (tiles, depth), 0)
    part_src[...] = jnp.zeros_like(part_src)
    share_list = to_partner(list_src, list_other, 0)
    share_part = to_partner(part_src, part_other, 1)
    own_half = cover.at[pl.ds(base, chips)]
    share_half = to_partner(own_half, own_half, 2)
    mean = None
    for step in range(ITERS):
        rows = []
        for t in range(tiles):
            cells = []
            for k in range(k_count):
                b = ids[k, t]
                cells.append(u[b // share, pl.ds(b % share, 1), :])
            rows.append(jnp.concatenate(cells, axis=1))
        lhs = pieces(jnp.concatenate(rows, axis=0))
        total = jnp.zeros((tiles, cols), jnp.float32)
        for p in range(pairs):
            if step == 0:
                loads[p].wait()
                for side in range(2):
                    w[p, :, side * cols : (side + 1) * cols] = (
                        inc_buf[2 * p + side].reshape(depth, cols).astype(jnp.float32).astype(jnp.bfloat16)
                    )
            got = fold(jnp.dot(lhs, w[p], preferred_element_type=jnp.float32))
            total = jnp.where(tile_row == 2 * p, got[:, :cols], total)
            total = jnp.where(tile_row == 2 * p + 1, got[:, cols:], total)
        if step == 0:
            pl.semaphore_wait(barrier, chips)
            share_list.start()
        reduced = costf - total
        scaled = reduced * 0.125
        primal = 1.0 / (1.0 + jnp.exp(scaled))
        mean = primal if step == 0 else 0.3 * primal + 0.7 * mean
        even = tile_row % 2 == 0
        lhs = pieces(
            jnp.concatenate([jnp.where(even, mean, 0.0), jnp.where(even, 0.0, mean)], axis=1)
        )
        part = jnp.zeros((tiles, depth), jnp.float32)
        for p in range(pairs):
            got = fold(
                lax.dot_general(
                    lhs, w[p], (((1,), (1,)), ((), ())), preferred_element_type=jnp.float32
                )
            )
            part = jnp.where(tile_row_wide // 2 == p, got, part)
        part = jnp.concatenate([part[:, k * blk : (k + 1) * blk] for k in range(k_count)], axis=0)
        soft = -8.0 * (jnp.maximum(-scaled, 0.0) + jnp.log1p(jnp.exp(-jnp.abs(scaled))))
        soft_row = jnp.sum(soft, axis=0, keepdims=True)
        if step > 0:
            share_part.wait_send()
        part_src[:count] = part
        part_src[count : count + 1] = soft_row
        share_part.start()
        if step > 0:
            wait_all(outgoing, rs_send)
            wait_all(cover, ag_send)
            share_half.wait_send()
        mine = jnp.dot(onehot[...], pieces(part), preferred_element_type=jnp.float32)
        if step == 0:
            share_list.wait_recv()
            other_onehot[...] = mark(list_other[...])
        share_part.wait_recv()
        mine = mine + jnp.dot(
            other_onehot[...], pieces(part_other[:count]), preferred_element_type=jnp.float32
        )
        outgoing[...] = mine.reshape(chips, share, blk)
        to_others(
            lambda d, where: pltpu.make_async_remote_copy(
                src_ref=outgoing.at[d], dst_ref=incoming.at[me],
                send_sem=rs_send, recv_sem=rs_recv,
                device_id=where, device_id_type=MESH,
            ).start()
        )
        soft_row = soft_row + part_other[count : count + 1]
        soft_src[step] = soft_row
        soft_buf[step, me] = soft_row
        to_others(
            lambda d, where: pltpu.make_async_remote_copy(
                src_ref=soft_src.at[step], dst_ref=soft_buf.at[step, me],
                send_sem=soft_send.at[step], recv_sem=soft_recv.at[step],
                device_id=where, device_id_type=MESH,
            ).start()
        )
        incoming[me] = outgoing[me]
        mult_sum = jnp.sum(u[...])
        wait_all(incoming, rs_recv)
        cover[base + me] = jnp.sum(incoming[...], axis=0)
        to_others(
            lambda d, where: pltpu.make_async_remote_copy(
                src_ref=cover.at[base + me], dst_ref=cover.at[base + me],
                send_sem=ag_send, recv_sem=ag_recv,
                device_id=where, device_id_type=MESH,
            ).start()
        )
        wait_all(soft_buf.at[step], soft_recv.at[step])
        value = mult_sum + jnp.sum(soft_buf[step])
        wait_all(cover, ag_recv)
        share_half.start()
        slope = 1.0 - cover[pl.ds(base, chips)]
        norm = jnp.sum(slope * slope)
        share_half.wait_recv()
        slope = 1.0 - cover[pl.ds(other_base, chips)]
        norm = norm + jnp.sum(slope * slope)
        size = (jnp.full((1, 1, blk), upper[0] - value)) / (norm + 1e-06)
        new = jnp.maximum(0.0, u[...] + size * (1.0 - cover[...]))
        if step < ITERS - 1:
            u[...] = new
        else:
            mult_out[...] = new
            mean_out[...] = mean
    wait_all(outgoing, rs_send)
    wait_all(cover, ag_send)
    for step in range(ITERS):
        wait_all(soft_buf.at[step], soft_send.at[step])
    share_list.wait_send()
    share_part.wait_send()
    share_half.wait_send()


def local(narrow, wide, block_ids, incidence, costs, start_mult, upper):
    n = narrow * wide
    tiles, k_count, blk, cols = incidence.shape
    blocks = start_mult.shape[0]
    share = blocks // n
    count = tiles * k_count
    f32 = jnp.float32
    vmem = pl.BlockSpec(memory_space=pltpu.VMEM)
    smem = pl.BlockSpec(memory_space=pltpu.SMEM)
    rows = (n, share, blk)
    half = (n // 2, share, blk)
    dma = pltpu.SemaphoreType.DMA
    mult, mean = pl.pallas_call(
        functools.partial(kernel, narrow, wide),
        name="volume",
        out_shape=(
            jax.ShapeDtypeStruct(rows, f32),
            jax.ShapeDtypeStruct(costs.shape, f32),
        ),
        in_specs=[smem, pl.BlockSpec(memory_space=pltpu.HBM), vmem, vmem, smem],
        out_specs=(vmem, vmem),
        scratch_shapes=[
            pltpu.VMEM(incidence.shape, jnp.int32),
            pltpu.VMEM((tiles // 2, k_count * blk, 2 * cols), jnp.bfloat16),
            pltpu.VMEM(rows, f32),
            pltpu.VMEM((blocks // 2, 3 * count), jnp.bfloat16),
            pltpu.VMEM((blocks // 2, 3 * count), jnp.bfloat16),
            pltpu.VMEM(half, f32),
            pltpu.VMEM(half, f32),
            pltpu.VMEM(rows, f32),
            pltpu.VMEM((count + 8, blk), f32),
            pltpu.VMEM((count + 8, blk), f32),
            pltpu.VMEM((1, 4 * count), f32),
            pltpu.VMEM((1, 4 * count), f32),
            pltpu.VMEM((ITERS, 1, cols), f32),
            pltpu.VMEM((ITERS, n // 2, 1, cols), f32),
            dma((tiles // 2,)), dma, dma, dma, dma, dma((ITERS,)), dma((ITERS,)), dma((3,)), dma((3,)),
        ],
        compiler_params=pltpu.CompilerParams(
            collective_id=0, has_side_effects=True, vmem_limit_bytes=52 * 2**20
        ),
    )(block_ids.T, incidence, costs, start_mult.reshape(rows), upper)
    return mult.reshape(blocks, blk), mean


def solution(mesh):
    in_specs = (
        P(("narrow", "wide"), None),
        P(("narrow", "wide"), None, None, None),
        P(("narrow", "wide"), None),
        P(),
        P(),
    )
    out_specs = (P(), P(("narrow", "wide"), None))
    body = functools.partial(local, mesh.shape["narrow"], mesh.shape["wide"])
    return jax.shard_map(body, mesh=mesh, in_specs=in_specs, out_specs=out_specs, check_vma=False)
```

time: 68.2 us -> 54.5 us (0.80)
  Pallas kernels: 62.3 us -> 49.3 us
  local copies, waits for them, and re-layouts: 4.32 us -> 3.62 us
    pallas_call x1, Pallas kernels: 62.3 us -> 49.3 us  [local(): pl.pallas_call(functools.partial(kernel, narrow, wide), name='volume', ou...]
    unnamed x3 -> x8, local copies, waits for them, and re-layouts: 4.32 us -> 3.62 us
where the time goes in v2:
time: 54.5 us; the launch traced here: 54.2 us
  Pallas kernels  49.3 us (90%)
  local copies, waits for them, and re-layouts  3.62 us (7%)
  between operations  1.3 us (2%)
    pallas_call x1, Pallas kernels, local(): pl.pallas_call(functools.partial(kernel, narrow, wide), name='volume', ou...  49.3 us
    unnamed x8, local copies, waits for them, and re-layouts  3.62 us

profile of v2, /device:TPU:0, one launch (start us, length us, event | category | flops | bytes accessed | tf_op | source)
XLA Modules:
  0.0 54.2 jit_solution(14302060994397789020)
XLA Ops:
  1.3 0.0 copy-start
  1.3 0.9 %copy-done = f32[512,128]{1,0:T(8,128)S(1)} copy-done((f32[512,128]{1,0:T(8,128)S(1)}, f32[512,128]{1,0:T(8,128)}, u32[]{:S(2)}) %copy-start) | copy-done | bytes 262168
  2.2 0.0 copy-start.1
  2.2 0.7 %copy-done.1 = s32[16,128]{1,0:T(8,128)S(1)} copy-done((s32[16,128]{1,0:T(8,128)S(1)}, s32[16,128]{1,0:T(8,128)}, u32[]{:S(2)}) %copy-start.1) | copy-done | bytes 8216
  2.9 0.0 copy-start.2
  2.9 0.7 %copy-done.2 = s32[16,4]{0,1:T(4,128)S(1)} copy-done((s32[16,4]{0,1:T(4,128)S(1)}, s32[16,4]{0,1:T(4,128)}, u32[]{:S(2)}) %copy-start.2) | copy-done | bytes 280
  3.6 49.3 %volume.1 = (f32[32,16,128]{2,1,0:T(8,128)S(1)}, f32[16,128]{1,0:T(8,128)S(1)}) custom-call(s32[4,16]{1,0:T(4,128)S(1)} %bitcast.5, s32[16,4,128,128]{3,2,1,0:T(8,128)} %inc.1, s32[16,128]{1,0:T(8,128)S(1)} %copy-done.1, f32[32,16,128]{2,1,0:T(8,128)S(1)} %bitcast.3, f32[1]{0:T(128)S(6)} %copy.9.upper), custom_call_target="tpu_custom_call" | custom-call | tf_op jit(solution)/shard_map/volume/pallas_call | solution.py:233
  52.9 0.7 %copy.10 = f32[512,128]{1,0:T(8,128)} copy(f32[512,128]{1,0:T(8,128)S(1)} %bitcast.4) | data formatting | bytes 524288
  53.6 0.6 %copy.11 = f32[16,128]{1,0:T(8,128)} copy(f32[16,128]{1,0:T(8,128)S(1)} %get-tuple-element.9) | data formatting | bytes 16384
Async XLA Ops:
  1.3 1.0 %copy-start = (f32[512,128]{1,0:T(8,128)S(1)}, f32[512,128]{1,0:T(8,128)}, u32[]{:S(2)}) copy-start(f32[512,128]{1,0:T(8,128)} %param.8) | copy-start | bytes 786436
  2.2 0.7 %copy-start.1 = (s32[16,128]{1,0:T(8,128)S(1)}, s32[16,128]{1,0:T(8,128)}, u32[]{:S(2)}) copy-start(s32[16,128]{1,0:T(8,128)} %costs.1) | copy-start | bytes 24580
  2.9 0.7 %copy-start.2 = (s32[16,4]{0,1:T(4,128)S(1)}, s32[16,4]{0,1:T(4,128)}, u32[]{:S(2)}) copy-start(s32[16,4]{0,1:T(4,128)} %param.5) | copy-start | bytes 772

commit v3 on v2

--- a/solution.py
+++ b/solution.py
@@ -46,14 +46,20 @@
     other_base = chips - base
 
     def to_others(act):
+        def go(d):
+            act(d, ((d // wide) * 2 + core, d % wide))
+
         def one(i, carry):
-            d = (me + i) % chips
-            act(d, ((d // wide) * 2 + core, d % wide))
+            go((me + i) % chips)
             return carry
 
-        if chips <= 16:
-            for i in range(1, chips):
-                one(i, 0)
+        if chips <= 16 and chips & (chips - 1) == 0:
+            for i in sorted(range(1, chips), key=lambda i: -i.bit_count()):
+                d = me
+                for bit in range(chips.bit_length() - 1):
+                    if (i >> bit) & 1:
+                        d = d + (1 << bit) * (1 - 2 * ((me // (1 << bit)) % 2))
+                go(d)
         else:
             lax.fori_loop(1, chips, one, 0)
 

time: 54.5 us -> 52.3 us (0.960)
  Pallas kernels: 49.3 us -> 47 us
    pallas_call x1, Pallas kernels: 49.3 us -> 47 us  [local(): pl.pallas_call(functools.partial(kernel, narrow, wide), name='volume', ou...]
where the time goes in v3:
time: 52.3 us; the launch traced here: 52 us
  Pallas kernels  47 us (90%)
  local copies, waits for them, and re-layouts  3.62 us (7%)
  between operations  1.3 us (2%)
    pallas_call x1, Pallas kernels, local(): pl.pallas_call(functools.partial(kernel, narrow, wide), name='volume', ou...  47 us
    unnamed x8, local copies, waits for them, and re-layouts  3.62 us

profile of v3, /device:TPU:0, one launch (start us, length us, event | category | flops | bytes accessed | tf_op | source)
XLA Modules:
  0.0 52.0 jit_solution(18026769463208798501)
XLA Ops:
  1.3 0.0 copy-start
  1.3 0.9 %copy-done = f32[512,128]{1,0:T(8,128)S(1)} copy-done((f32[512,128]{1,0:T(8,128)S(1)}, f32[512,128]{1,0:T(8,128)}, u32[]{:S(2)}) %copy-start) | copy-done | bytes 262168
  2.2 0.0 copy-start.1
  2.2 0.7 %copy-done.1 = s32[16,128]{1,0:T(8,128)S(1)} copy-done((s32[16,128]{1,0:T(8,128)S(1)}, s32[16,128]{1,0:T(8,128)}, u32[]{:S(2)}) %copy-start.1) | copy-done | bytes 8216
  2.9 0.0 copy-start.2
  2.9 0.7 %copy-done.2 = s32[16,4]{0,1:T(4,128)S(1)} copy-done((s32[16,4]{0,1:T(4,128)S(1)}, s32[16,4]{0,1:T(4,128)}, u32[]{:S(2)}) %copy-start.2) | copy-done | bytes 280
  3.6 47.0 %volume.1 = (f32[32,16,128]{2,1,0:T(8,128)S(1)}, f32[16,128]{1,0:T(8,128)S(1)}) custom-call(s32[4,16]{1,0:T(4,128)S(1)} %bitcast.5, s32[16,4,128,128]{3,2,1,0:T(8,128)} %inc.1, s32[16,128]{1,0:T(8,128)S(1)} %copy-done.1, f32[32,16,128]{2,1,0:T(8,128)S(1)} %bitcast.3, f32[1]{0:T(128)S(6)} %copy.9.upper), custom_call_target="tpu_custom_call" | custom-call | tf_op jit(solution)/shard_map/volume/pallas_call | solution.py:239
  50.6 0.7 %copy.10 = f32[512,128]{1,0:T(8,128)} copy(f32[512,128]{1,0:T(8,128)S(1)} %bitcast.4) | data formatting | bytes 524288
  51.4 0.6 %copy.11 = f32[16,128]{1,0:T(8,128)} copy(f32[16,128]{1,0:T(8,128)S(1)} %get-tuple-element.9) | data formatting | bytes 16384
Async XLA Ops:
  1.3 1.0 %copy-start = (f32[512,128]{1,0:T(8,128)S(1)}, f32[512,128]{1,0:T(8,128)}, u32[]{:S(2)}) copy-start(f32[512,128]{1,0:T(8,128)} %param.8) | copy-start | bytes 786436
  2.2 0.7 %copy-start.1 = (s32[16,128]{1,0:T(8,128)S(1)}, s32[16,128]{1,0:T(8,128)}, u32[]{:S(2)}) copy-start(s32[16,128]{1,0:T(8,128)} %costs.1) | copy-start | bytes 24580
  2.9 0.7 %copy-start.2 = (s32[16,4]{0,1:T(4,128)S(1)}, s32[16,4]{0,1:T(4,128)}, u32[]{:S(2)}) copy-start(s32[16,4]{0,1:T(4,128)} %param.5) | copy-start | bytes 772
